TPU v7x, 32 devices: a whole 2x2x4 slice. The times are simulated.
32 devices in a mesh: seq: 8 (over y, x, core), tp: 4 (over z).
Axes of the slice: x: 2, y: 2, z: 4, core: 2. Of those that a mesh axis runs over, the one named last changes fastest.
Arguments:
- states: bfloat16 [8, 128, 2048], P('seq', None, 'tp'), may hold values from -60 to 60, as said below
- cotangent: bfloat16 [8, 128, 2048], P('seq', None, 'tp'), may hold values from -12 to 12, as said below
- wq: bfloat16 [2048, 2048], P(None, 'tp'), may hold values from -0.125 to 0.125
- wk: bfloat16 [2048, 512], P(None, 'tp'), may hold values from -0.125 to 0.125
- wv: bfloat16 [2048, 512], P(None, 'tp'), may hold values from -0.125 to 0.125
- wo: bfloat16 [2048, 2048], P('tp'), may hold values from -0.125 to 0.125
Outputs:
- gram: float32 [8, 8], P('seq')
Inputs may be any that keep to these rules, and one draw needn't show every extreme that they name: `states`: finite values. `cotangent`: finite values.
All inputs are finite; a program needn't handle non-finite values.
Results may differ from a plain program's by a relative error of at most 0.0025.
Values may be sent and summed in bfloat16 or wider, within the bound.
A program may use at most 64 MiB of HBM per device.

v0:
```python
import jax
import jax.numpy as jnp
from jax import lax
from jax.sharding import PartitionSpec as P

HEADS = 32
KV_HEADS = 8
HEAD_DIM = 64


theta_base = 500000.0


def from_behind(block, axis, distance):
    devices = range(lax.axis_size(axis))
    route = [((i - distance) % len(devices), i) for i in devices]
    return lax.ppermute(block, axis, route)


def rope_tables(length, head_dim):
    half_dim = head_dim // 2
    freqs_k = theta_base ** (-(jnp.arange(half_dim, dtype=jnp.float32) * 2.0 / head_dim))
    angles = jnp.arange(length, dtype=jnp.float32)[:, None] * freqs_k[None, :]
    angles = jnp.concatenate([angles, angles], axis=1)
    return (jnp.cos(angles)[:, None, :], jnp.sin(angles)[:, None, :])


def rotate(values_in, cos_table, sine_table):
    half_dim = values_in.shape[-1] // 2
    turned = jnp.concatenate([-values_in[..., half_dim:], values_in[..., :half_dim]], axis=-1)
    return values_in * cos_table + turned * sine_table


def attention_factors(states, cotangent, wq, wk, wv, wo):
    seq_dev, length, part_width = states.shape
    full_states, full_cot = (
        lax.all_gather(states, "tp", axis=2, tiled=True),
        lax.all_gather(cotangent, "tp", axis=2, tiled=True),
    )
    model_width = full_states.shape[2]
    tok_rows = seq_dev * length
    kv_local = wk.shape[1] // HEAD_DIM
    group_size = HEADS // KV_HEADS
    cos_table, sine_table = rope_tables(length, HEAD_DIM)
    flat_states = full_states.reshape(tok_rows, model_width)
    query_heads = jnp.dot(flat_states, wq, preferred_element_type=jnp.float32).reshape(
        seq_dev, length, kv_local * group_size, HEAD_DIM
    )
    query_heads = (
        rotate(query_heads, cos_table, sine_table)
        .astype(jnp.bfloat16)
        .reshape(seq_dev, length, kv_local, group_size, HEAD_DIM)
    )
    key_heads = jnp.dot(flat_states, wk, preferred_element_type=jnp.float32).reshape(
        seq_dev, length, kv_local, HEAD_DIM
    )
    key_heads = rotate(key_heads, cos_table, sine_table).astype(jnp.bfloat16)
    value_heads = (
        jnp.dot(flat_states, wv, preferred_element_type=jnp.float32)
        .astype(jnp.bfloat16)
        .reshape(seq_dev, length, kv_local, HEAD_DIM)
    )
    scores = jnp.einsum(
        "sqkgd,stkd->skgqt", query_heads, key_heads, preferred_element_type=jnp.float32
    ) * HEAD_DIM ** (-0.5)
    causal = jnp.arange(length)[:, None] >= jnp.arange(length)[None, :]
    scores = jnp.where(causal, scores, -jnp.inf)
    weights_bf = jax.nn.softmax(scores, axis=-1).astype(jnp.bfloat16)
    attended = (
        jnp.einsum("skgqt,stkd->sqkgd", weights_bf, value_heads, preferred_element_type=jnp.float32)
        .astype(jnp.bfloat16)
        .reshape(tok_rows, part_width)
    )
    grad_attended = (
        lax.dot_general(
            full_cot.reshape(tok_rows, model_width),
            wo,
            (((1,), (1,)), ((), ())),
            preferred_element_type=jnp.float32,
        )
        .astype(jnp.bfloat16)
        .reshape(seq_dev, length, kv_local, group_size, HEAD_DIM)
    )
    value_gradient = (
        jnp.einsum(
            "skgqt,sqkgd->stkd", weights_bf, grad_attended, preferred_element_type=jnp.float32
        )
        .astype(jnp.bfloat16)
        .reshape(tok_rows, kv_local * HEAD_DIM)
    )
    return jnp.concatenate(
        [
            states.reshape(tok_rows, part_width),
            attended,
            cotangent.reshape(tok_rows, part_width),
            value_gradient,
        ],
        axis=1,
    )


def tile_of(left_rows, right_rows, begin_col, end_col):
    return lax.dot_general(
        left_rows[:, begin_col:end_col],
        right_rows[:, begin_col:end_col],
        (((1,), (1,)), ((), ())),
        preferred_element_type=jnp.float32,
    )


def pair_block(own_rows, other_rows, part_width, seq_dev, length):
    tiles = jnp.stack(
        [
            tile_of(own_rows, other_rows, 0, part_width),
            tile_of(own_rows, other_rows, part_width, 2 * part_width),
            tile_of(own_rows, other_rows, 2 * part_width, 3 * part_width),
            tile_of(own_rows, other_rows, 3 * part_width, own_rows.shape[1]),
        ]
    )
    shares = lax.psum_scatter(
        tiles.astype(jnp.bfloat16), "tp", scatter_dimension=1, tiled=True
    ).astype(jnp.float32)
    product = shares[0] * shares[3] + shares[1] * shares[2]
    share_rows = product.shape[0]
    col_sums = product.reshape(share_rows, seq_dev, length).sum(axis=2)
    first_row = lax.axis_index("tp") * share_rows
    row_seq = (first_row + jnp.arange(share_rows, dtype=jnp.int32)) // length
    member = (row_seq[None, :] == jnp.arange(seq_dev, dtype=jnp.int32)[:, None]).astype(jnp.float32)
    return jnp.dot(member, col_sums, precision=lax.Precision.HIGHEST)


def record(totals, block, distance, me_index, n_seq, half_rotation):
    row_acc, col_acc = totals
    seq_dev = block.shape[0]
    distance = jnp.asarray(distance, jnp.int32)
    offset = (me_index + distance) % n_seq * seq_dev
    zero_at = jnp.zeros((), jnp.int32)
    row_on = jnp.where(distance < half_rotation, 1.0, 0.0).astype(jnp.float32)
    row_acc = lax.dynamic_update_slice(row_acc, block * row_on, (zero_at, offset))
    mirror_on = jnp.where((distance > 0) & (distance <= half_rotation), 1.0, 0.0).astype(
        jnp.float32
    )
    col_acc = lax.dynamic_update_slice(col_acc, block.T * mirror_on, (offset, zero_at))
    return (row_acc, col_acc)


def on_device(states, cotangent, wq, wk, wv, wo):
    seq_dev, length, part_width = states.shape
    own_rows = attention_factors(states, cotangent, wq, wk, wv, wo)
    n_seq = lax.axis_size("seq")
    half_rotation = n_seq // 2
    me_index = lax.axis_index("seq")
    totals = (
        jnp.zeros((seq_dev, n_seq * seq_dev), jnp.float32),
        jnp.zeros((n_seq * seq_dev, seq_dev), jnp.float32),
    )

    def measure(totals_in, other_rows, distance):
        block = pair_block(own_rows, other_rows, part_width, seq_dev, length)
        return record(totals_in, block, distance, me_index, n_seq, half_rotation)

    totals = measure(totals, own_rows, 0)
    near_count = half_rotation // 2
    far_count = half_rotation - 1 - near_count
    opposite = from_behind(own_rows, "seq", half_rotation)
    totals = measure(totals, opposite, half_rotation)

    def near_turn(visitor, totals_in, distance):
        visitor = from_behind(visitor, "seq", -1)
        return (visitor, measure(totals_in, visitor, distance))

    def paired_turn(step_index, carried):
        near_rows, far_rows, totals_in = carried
        near_rows, totals_in = near_turn(near_rows, totals_in, step_index + 1)
        far_rows = from_behind(far_rows, "seq", 1)
        return (near_rows, far_rows, measure(totals_in, far_rows, half_rotation - 1 - step_index))

    near_rows, far_rows, totals = lax.fori_loop(
        0, far_count, paired_turn, (own_rows, opposite, totals)
    )
    near_rows, totals = near_turn(near_rows, totals, near_count)
    row_acc, col_acc = lax.psum((totals[0], totals[1]), "tp")
    mirrored = lax.all_to_all(col_acc, "seq", split_axis=0, concat_axis=1, tiled=True)
    kernel = row_acc + mirrored
    own_block = lax.dynamic_slice_in_dim(kernel, me_index * seq_dev, seq_dev, 1)
    own_diag = jnp.diagonal(own_block)
    all_diag = lax.all_gather(own_diag, "seq", axis=0, tiled=True)
    return kernel / jnp.sqrt(own_diag[:, None] * all_diag[None, :])


def solution(mesh):
    in_specs = (
        P("seq", None, "tp"),
        P("seq", None, "tp"),
        P(None, "tp"),
        P(None, "tp"),
        P(None, "tp"),
        P("tp", None),
    )
    out_specs = P("seq", None)
    return jax.shard_map(
        on_device, mesh=mesh, in_specs=in_specs, out_specs=out_specs, check_vma=False
    )
```

profile of v0, /device:TPU:0, one launch (start us, length us, event | category | flops | bytes accessed | tf_op | source)
XLA Modules:
  0.0 167.4 jit_solution(4516252075770573431)
XLA Ops:
  6.7 17.7 %all_gather.9 = bf16[1,128,2048]{2,1,0:T(8,128)(2,1)S(1)} all-gather(bf16[1,128,512]{2,1,0:T(8,128)(2,1)} %param.6), channel_id=1, replica_groups=mesh['seq'=8,'tp'=4] {'tp'}, dimensions={2}, use_global_device_ids=true | all-gather | bytes 655360 | tf_op jit(solution)/shard_map/all_gather | solution.py:37
  24.4 1.4 convolution_convert_fusion.19
  25.8 1.4 fusion.28
  27.2 0.9 fusion.26
  28.3 0.3 fusion.88
  28.8 0.2 convolution_convert_fusion.1
  29.1 16.4 %all_gather.10 = bf16[1,128,2048]{2,1,0:T(8,128)(2,1)S(1)} all-gather(bf16[1,128,512]{2,1,0:T(8,128)(2,1)S(1)} %copy-done.1), channel_id=1, replica_groups=mesh['seq'=8,'tp'=4] {'tp'}, dimensions={2}, use_global_device_ids=true | all-gather | bytes 655360 | tf_op jit(solution)/shard_map/all_gather | solution.py:38
  45.5 2.4 %convolution_convert_fusion = bf16[128,512]{1,0:T(8,128)(2,1)S(1)} fusion(bf16[512,2048]{1,0:T(8,128)(2,1)} %param.11, bf16[1,128,2048]{2,1,0:T(8,128)(2,1)S(1)} %all_gather.10), kind=kOutput, calls=%fused_computation.3 | convolution fusion | flops 268500992 | bytes 2752512 | tf_op jit(solution)/shard_map/dot_general | solution.py:75
  48.0 0.2 fusion.2
  48.5 1.6 collective-permute-start
  50.1 0.2 fusion.5
  50.3 0.2 fusion.23
  50.4 0.2 fusion.6
  50.6 0.2 fusion.24
  50.9 0.7 pad_maximum_fusion.1
  51.6 2.6 %collective-permute-done.1 = bf16[128,1664]{1,0:T(8,128)(2,1)} collective-permute-done((bf16[128,1664]{1,0:T(8,128)(2,1)S(1)}, bf16[128,1664]{1,0:T(8,128)(2,1)}, u32[]{:S(2)}, u32[]{:S(2)}) %collective-permute-start.1) | collective-permute-done | bytes 426016 | tf_op jit(solution)/shard_map/while/body/eval_jaxpr/ppermute | solution.py:17
  54.2 1.1 fusion.10
  55.3 0.9 fusion.18
  56.2 1.1 fusion.17
  57.2 1.1 fusion.9
  58.4 0.8 copy.71
  59.2 3.0 %collective-permute-start.3 = (bf16[128,1664]{1,0:T(8,128)(2,1)}, bf16[128,1664]{1,0:T(8,128)(2,1)}, u32[]{:S(2)}, u32[]{:S(2)}) collective-permute-start(bf16[128,1664]{1,0:T(8,128)(2,1)} %collective-permute-done.1), channel_id=1, source_target_pairs={{4,0},{8,4},{12,8},{16,12},{20,16},{24,20},{28,24},{0,28},{5,1},{9... | collective-permute-start | bytes 1277960 | tf_op jit(solution)/shard_map/ppermute | solution.py:17
  62.1 0.2 fusion.8
  62.4 0.2 fusion.15
  62.6 0.2 fusion.7
  62.9 0.8 copy.68
  63.7 4.4 %collective-permute-done.3 = bf16[128,1664]{1,0:T(8,128)(2,1)} collective-permute-done((bf16[128,1664]{1,0:T(8,128)(2,1)}, bf16[128,1664]{1,0:T(8,128)(2,1)}, u32[]{:S(2)}, u32[]{:S(2)}) %collective-permute-start.3) | collective-permute-done | bytes 426016 | tf_op jit(solution)/shard_map/ppermute | solution.py:17
  68.1 1.1 fusion.14
  69.2 0.9 fusion.22
  70.1 1.1 fusion.21
  71.2 1.1 fusion.13
  72.3 2.3 %collective-permute-done.2 = bf16[128,1664]{1,0:T(8,128)(2,1)S(1)} collective-permute-done((bf16[128,1664]{1,0:T(8,128)(2,1)S(1)}, bf16[128,1664]{1,0:T(8,128)(2,1)S(1)}, u32[]{:S(2)}, u32[]{:S(2)}) %collective-permute-start.2) | collective-permute-done | bytes 426016 | tf_op jit(solution)/shard_map/while/body/eval_jaxpr/ppermute | solution.py:17
  74.8 0.2 fusion.12
  75.1 0.8 copy.77
  75.9 0.2 fusion.11
  76.1 0.8 copy.74
  77.0 0.6 dynamic-slice.1
  78.3 0.8 convert_element_type.81
  79.2 0.6 select_reduce_fusion.4
  80.5 0.7 dynamic_update_slice.34
  81.2 34.0 %all-reduce.9.cloned.1.call-done = (bf16[4,128,128]{2,0,1:T(4,128)(2,1)}, bf16[4,128,128]{2,0,1:T(4,128)(2,1)}, bf16[4,128,128]{2,0,1:T(4,128)(2,1)}, bf16[4,128,128]{2,0,1:T(4,128)(2,1)}) async-done(((bf16[4,128,128]{2,0,1:T(4,128)(2,1)}, bf16[4,128,128]{2,0,1:T(4,128)(2,1)}, bf16[4,128,128]{2,0,1:T(4,128)(2,1)}, bf16[4,128,128]{2,0,1:T(4,128)(2,1)}), (bf16[4,128,128]{2,0,1:T(4,128)(2,1)}, ...) | async-done | bytes 524304
  115.2 0.8 dynamic-slice_convert_fusion.3
  116.0 0.3 fusion.72
  116.3 0.8 dynamic-slice_convert_fusion.2
  117.1 0.3 fusion.73
  117.4 0.7 select_reduce_fusion.2
  118.7 0.8 dynamic-slice_convert_fusion.1
  119.5 0.8 dynamic-slice_convert_fusion
  120.3 0.3 fusion.75
  120.6 0.3 fusion.74
  121.0 0.6 constant_dynamic-update-slice_fusion.3
  121.7 0.7 constant_dynamic-update-slice_fusion.2
  122.3 0.8 dynamic_update_slice.36
  123.1 0.7 select_reduce_fusion
  123.8 0.8 dynamic_update_slice.37
  124.6 0.7 constant_dynamic-update-slice_fusion.1
  125.3 0.7 constant_dynamic-update-slice_fusion
  125.9 0.8 dynamic_update_slice.38
  126.7 0.6 dynamic-slice
  127.3 10.7 %all-reduce.5 = (f32[1,8]{1,0:T(1,128)S(1)}, f32[8,1,1]{2,1,0:T(1,128)S(1)}) all-reduce(f32[1,8]{1,0:T(1,128)S(1)} %dynamic_update_slice.38, f32[8,1,1]{2,1,0:T(1,128)S(1)} %constant_dynamic-update-slice_fusion), channel_id=1, replica_groups=mesh['seq'=8,'tp'=4] {'tp'}, use_global_device_ids=true, to_apply=%region_12.13 | all-reduce | flops 16 | bytes 128 | tf_op jit(solution)/shard_map/psum | solution.py:182
  138.0 8.1 %all_to_all.16 = f32[8,1,1]{2,1,0:T(1,128)S(1)} all-to-all(f32[8,1,1]{2,1,0:T(1,128)S(1)} %get-tuple-element.26), channel_id=1, replica_groups=mesh['seq'=8,'tp'=4] {'seq'}, dimensions={0} | all-to-all | bytes 64 | tf_op jit(solution)/shard_map/all_to_all | solution.py:183
  146.2 1.3 bitcast_dynamic-update-slice_fusion
  147.5 11.8 %all-reduce = f32[8]{0:T(128)S(1)} all-reduce(f32[8]{0:T(128)S(1)} %get-tuple-element.52), channel_id=2, replica_groups=mesh['seq'=8,'tp'=4] {'seq'}, use_global_device_ids=true, to_apply=%add | all-reduce | flops 8 | bytes 64
  159.3 1.2 bitcast_multiply_fusion
  (45 shorter events, 1.9 us)
Async XLA Ops:
  6.5 20.7 %copy-start = (bf16[2048,512]{1,0:T(8,128)(2,1)S(1)}, bf16[2048,512]{1,0:T(8,128)(2,1)}, u32[]{:S(2)}) copy-start(bf16[2048,512]{1,0:T(8,128)(2,1)} %param.8) | copy-start | bytes 6291460
  6.5 71.8 %reduce-scatter.2.cloned.1.call-start = ((), (), s32[]{:S(2)}) async-start(), calls=%async_computation.2 | async-start | bytes 163840 | tf_op jit(solution)/shard_map/reduce_scatter | solution.py:120
  28.2 0.9 copy-start.1
  29.1 19.3 %copy-start.2 = (bf16[1,128,512]{2,1,0:T(8,128)(2,1)S(1)}, bf16[1,128,512]{2,1,0:T(8,128)(2,1)}, u32[]{:S(2)}) copy-start(bf16[1,128,512]{2,1,0:T(8,128)(2,1)} %param.6) | copy-start | bytes 393220
  48.4 5.7 %collective-permute-start.1 = (bf16[128,1664]{1,0:T(8,128)(2,1)S(1)}, bf16[128,1664]{1,0:T(8,128)(2,1)}, u32[]{:S(2)}, u32[]{:S(2)}) collective-permute-start(bf16[128,1664]{1,0:T(8,128)(2,1)S(1)} %pad_maximum_fusion), channel_id=1, source_target_pairs={{4,0},{8,4},{12,8},{16,12},{20,16},{24,20},{28,24},{0,28},{5,1},{9... | collective-permute-start | bytes 1277960 | tf_op jit(solution)/shard_map/while/body/eval_jaxpr/ppermute | solution.py:17
  48.5 13.6 %collective-permute-start = (bf16[128,1664]{1,0:T(8,128)(2,1)S(1)}, bf16[128,1664]{1,0:T(8,128)(2,1)S(1)}, u32[]{:S(2)}, u32[]{:S(2)}) collective-permute-start(bf16[128,1664]{1,0:T(8,128)(2,1)S(1)} %pad_maximum_fusion), channel_id=1, source_target_pairs={{16,0},{20,4},{24,8},{28,12},{0,16},{4,20},{8,24},{12,28},{17,1},{... | collective-permute-start | bytes 1277960 | tf_op jit(solution)/shard_map/ppermute | solution.py:17
  51.6 63.7 %all-reduce.9.cloned.1.call-start = ((), (), s32[]{:S(2)}) async-start(), calls=%async_computation.3 | async-start | bytes 1048576
  59.2 8.9 %collective-permute-start.3 = (bf16[128,1664]{1,0:T(8,128)(2,1)}, bf16[128,1664]{1,0:T(8,128)(2,1)}, u32[]{:S(2)}, u32[]{:S(2)}) collective-permute-start(bf16[128,1664]{1,0:T(8,128)(2,1)} %collective-permute-done.1), channel_id=1, source_target_pairs={{4,0},{8,4},{12,8},{16,12},{20,16},{24,20},{28,24},{0,28},{5,1},{9... | collective-permute-start | bytes 1277960 | tf_op jit(solution)/shard_map/ppermute | solution.py:17
  62.8 14.2 %copy-start.4 = (u32[32]{0:T(128)S(1)}, u32[32]{0:T(128)}, u32[]{:S(2)}) copy-start(u32[32]{0:T(128)} %constant.159) | copy-start | bytes 388
  63.7 11.0 %collective-permute-start.2 = (bf16[128,1664]{1,0:T(8,128)(2,1)S(1)}, bf16[128,1664]{1,0:T(8,128)(2,1)S(1)}, u32[]{:S(2)}, u32[]{:S(2)}) collective-permute-start(bf16[128,1664]{1,0:T(8,128)(2,1)S(1)} %collective-permute-done), channel_id=1, source_target_pairs={{28,0},{0,4},{4,8},{8,12},{12,16},{16,20},{20,24},{24,28},{29,1},{... | collective-permute-start | bytes 1277960 | tf_op jit(solution)/shard_map/while/body/eval_jaxpr/ppermute | solution.py:17
  70.1 56.6 %copy-start.3 = (u32[32]{0:T(128)S(1)}, u32[32]{0:T(128)}, u32[]{:S(2)}) copy-start(u32[32]{0:T(128)} %constant.143) | copy-start | bytes 388
Sparse Core Ops, SparseCore 0:
  51.7 18.9 reduce-scatter.1
  77.1 38.1 all-reduce.8
where the time goes:
time: 168 us; the launch traced here: 167 us
  blocking collectives  64.7 us (39%)
  waiting for transfers between devices  43.4 us (26%)
  matrix products  17.2 us (10%)
  between operations  15.8 us (9%)
  local copies, waits for them, and re-layouts  11.8 us (7%)
  other arithmetic  9.77 us (6%)
  starting transfers between devices  4.64 us (3%)
    unnamed x3, waiting for transfers between devices  34.1 us
    all_gather x1, blocking collectives, attention_factors(): lax.all_gather(states, 'tp', axis=2, tiled=True)  17.7 us
    all_gather x1, blocking collectives, attention_factors(): lax.all_gather(cotangent, 'tp', axis=2, tiled=True)  16.4 us
    unnamed x1, blocking collectives  11.8 us
    psum x1, blocking collectives, on_device(): row_acc, col_acc = lax.psum((totals[0], totals[1]), 'tp')  10.7 us
    dot_general x20, matrix products, tile_of(): lax.dot_general(left_rows[:, begin_col:end_col], right_rows[:, begin_col:...  10.4 us
    ppermute x4, waiting for transfers between devices, from_behind(): return lax.ppermute(block, axis, route)  9.32 us
    all_to_all x1, blocking collectives, on_device(): lax.all_to_all(col_acc, 'seq', split_axis=0, concat_axis=1, tiled=True)  8.08 us
  transfers between devices with their start and end apart: 6, of which 4 were waited for; matrix products, arithmetic and copies ran while one was open for 10% of the time, Pallas kernels for 0%

commit v1 on v0

v1 whole, which is shorter than its diff:
```python
import functools

import jax
import jax.numpy as jnp
import numpy as np
from jax import lax
from jax.experimental import pallas as pl
from jax.experimental.pallas import tpu as pltpu
from jax.sharding import PartitionSpec as P

HEADS = 32
KV_HEADS = 8
HEAD_DIM = 64
THETA = 500000.0
LANES = 128
GROUP = HEADS // KV_HEADS
F32, BF16 = jnp.float32, jnp.bfloat16

NT = (((1,), (1,)), ((), ()))
TN = (((0,), (0,)), ((), ()))


def rope_tables(length):
    half = HEAD_DIM // 2
    freqs = np.float32(THETA) ** (-(np.arange(half, dtype=np.float32) * np.float32(2.0 / HEAD_DIM)))
    angles = np.arange(length, dtype=np.float32)[:, None] * freqs[None, :].astype(np.float32)
    cos, sin = np.cos(angles), np.sin(angles)
    return (
        np.concatenate([cos, cos] * 2, axis=1).astype(np.float32),
        np.concatenate([-sin, sin] * 2, axis=1).astype(np.float32),
    )


def dot(a, b, dims=None):
    if dims is None:
        return jnp.dot(a, b, preferred_element_type=F32)
    return lax.dot_general(a, b, dims, preferred_element_type=F32)


def place_of(index, n):
    if n % 8:
        return index
    block, rest = index // 8, index % 8
    row, col, core = rest // 4, (rest // 2) % 2, rest % 2
    return block * 8 + 2 * (2 * row + (row + col) % 2) + core


def index_at(place, n):
    if n % 8:
        return place
    block, rest = place // 8, place % 8
    spot, core = rest // 2, rest % 2
    row = spot // 2
    return block * 8 + 2 * (2 * row + (row + spot) % 2) + core


def kernel(
    n, tp,
    states_ref, cot_ref, cos_ref, sin_ref, wq_hbm, wk_hbm, wv_hbm, wo_hbm,
    out_ref,
    xs, cs, wqb, wkb, wvb, wob, q_acc, k_acc, v_acc, g_acc,
    fs, fc, fac, fin, ad, rs, full, t1, t1_in, t2,
    w_sem, x_snd, x_rcv, p_snd, p_rcv, f_snd, f_rcv,
    rs_snd, rs_rcv, ag_snd, ag_rcv, r1_snd, r1_rcv, r2_snd, r2_rcv,
):
    length, width = states_ref.shape
    kv_cols = k_acc.shape[1]
    half = n // 2
    rows = length // tp
    lanes = t1.shape[1]
    me = lax.axis_index("seq")
    col = lax.axis_index("tp")
    place = place_of(me, n)

    def turn(d):
        return d * (1 - 2 * ((d + 1) % 2))

    def source(d):
        return index_at((place + turn(d) + n) % n, n)

    def target(d):
        return index_at((place - turn(d) + n) % n, n)

    def peer(k):
        return (col + k) % tp

    def each(lo, hi, body):
        if hi - lo <= 8:
            for i in range(lo, hi):
                body(i)
        else:
            lax.fori_loop(lo, hi, lambda i, c: (body(i), c)[1], 0)

    weight_copies = []
    for k in range(tp):
        at = pl.ds(pl.multiple_of(((col - k + tp) % tp) * width, width), width)
        copies = [
            pltpu.make_async_copy(wq_hbm.at[at, :], wqb.at[k], w_sem.at[4 * k]),
            pltpu.make_async_copy(wk_hbm.at[at, :], wkb.at[k], w_sem.at[4 * k + 1]),
            pltpu.make_async_copy(wv_hbm.at[at, :], wvb.at[k], w_sem.at[4 * k + 2]),
            pltpu.make_async_copy(wo_hbm.at[:, at], wob.at[k], w_sem.at[4 * k + 3]),
        ]
        weight_copies.append(copies)

    barrier = pltpu.get_barrier_semaphore()
    for k in range(1, tp):
        pl.semaphore_signal(barrier, inc=1, device_id={"tp": peer(k)})
    each(1, n, lambda o: pl.semaphore_signal(barrier, inc=1, device_id={"seq": (me + o) % n}))
    for copies in weight_copies:
        for c in copies:
            c.start()
    pl.semaphore_wait(barrier, tp - 1 + n - 1)

    def remote(src, dst, snd, rcv, device):
        return pltpu.make_async_remote_copy(
            src_ref=src, dst_ref=dst, send_sem=snd, recv_sem=rcv, device_id=device
        )

    order = sorted(range(1, tp), key=lambda k: min(k, tp - k))
    x_copies = {}
    for k in order:
        to = {"tp": peer(k)}
        x_copies[k] = (
            remote(states_ref, xs.at[k - 1], x_snd.at[0, k - 1], x_rcv.at[0, k - 1], to),
            remote(cot_ref, cs.at[k - 1], x_snd.at[1, k - 1], x_rcv.at[1, k - 1], to),
        )
        for c in x_copies[k]:
            c.start()

    def plane_copies(d):
        to = {"seq": target(d)}
        return (
            remote(states_ref, fs.at[d - 1], p_snd.at[0, d - 1], p_rcv.at[0, d - 1], to),
            remote(cot_ref, fc.at[d - 1], p_snd.at[1, d - 1], p_rcv.at[1, d - 1], to),
        )

    def start_plane(d):
        for c in plane_copies(d):
            c.start()

    each(1, half + 1, start_plane)

    for k in [0] + order:
        for c in weight_copies[k]:
            c.wait()
        if k == 0:
            x, y = states_ref[...], cot_ref[...]
        else:
            for c in x_copies[k]:
                c.wait_recv()
            x, y = xs[k - 1], cs[k - 1]
        for acc, piece in (
            (q_acc, dot(x, wqb[k])),
            (k_acc, dot(x, wkb[k])),
            (v_acc, dot(x, wvb[k])),
            (g_acc, dot(y, wob[k], NT)),
        ):
            if k == 0:
                acc[...] = piece
            else:
                acc[...] += piece

    lane = lax.broadcasted_iota(jnp.int32, (length, LANES), 1)
    low = lane < HEAD_DIM
    first = lane % HEAD_DIM < HEAD_DIM // 2
    cos, sin = cos_ref[...], sin_ref[...]
    causal = lax.broadcasted_iota(jnp.int32, (length, length), 0) >= lax.broadcasted_iota(
        jnp.int32, (length, length), 1
    )

    def swap(v):
        return pltpu.roll(v, HEAD_DIM, 1)

    def rope(v):
        turned = jnp.where(
            first, pltpu.roll(v, LANES - HEAD_DIM // 2, 1), pltpu.roll(v, HEAD_DIM // 2, 1)
        )
        return v * cos + turned * sin

    def halves(v):
        other = swap(v)
        zero = jnp.zeros_like(v)
        return (
            (jnp.where(low, v, zero).astype(BF16), jnp.where(low, zero, other).astype(BF16)),
            (jnp.where(low, other, zero).astype(BF16), jnp.where(low, zero, v).astype(BF16)),
        )

    def attention():
        for b in range(kv_cols // LANES):
            kcut = slice(b * LANES, (b + 1) * LANES)
            keys = halves(rope(k_acc[:, kcut]))
            values = halves(v_acc[:, kcut])
            sums = []
            for g in range(2):
                parts = [None, None]
                for pair in range(GROUP // 2):
                    at = ((b * 2 + g) * (GROUP // 2) + pair) * LANES
                    cut = slice(at, at + LANES)
                    q = rope(q_acc[:, cut]).astype(BF16)
                    ga = g_acc[:, cut].astype(BF16)
                    att = None
                    for side in range(2):
                        s = dot(q, keys[g][side], NT) * HEAD_DIM ** (-0.5)
                        s = jnp.where(causal, s, -jnp.inf)
                        e = jnp.exp(s - jnp.max(s, axis=1, keepdims=True))
                        p = (e / jnp.sum(e, axis=1, keepdims=True)).astype(BF16)
                        a = dot(p, values[g][side])
                        att = a if att is None else att + a
                        u = dot(p, ga, TN)
                        parts[side] = u if parts[side] is None else parts[side] + u
                    fac[:, cut] = att.astype(BF16)
                sums.append(parts)
            grad = jnp.where(
                low, sums[0][0] + swap(sums[0][1]), swap(sums[1][0]) + sums[1][1]
            )
            fac[:, width + b * LANES : width + (b + 1) * LANES] = grad.astype(BF16)

    def fac_copy(d):
        return remote(
            fac, fin.at[d - 1], f_snd.at[d - 1], f_rcv.at[d - 1], {"seq": target(d)}
        )

    def band(k):
        return pl.ds(pl.multiple_of(k * rows, rows), rows)

    def own_pairs():
        ad[0] = dot(states_ref[...], states_ref[...], NT).astype(BF16)
        ad[1] = dot(cot_ref[...], cot_ref[...], NT).astype(BF16)

        def pair(d):
            for c in plane_copies(d):
                c.wait_recv()
            ad[2 * d] = dot(states_ref[...], fs[d - 1], NT).astype(BF16)
            ad[2 * d + 1] = dot(cot_ref[...], fc[d - 1], NT).astype(BF16)

        each(1, half + 1, pair)

    rs_copies = [
        remote(
            ad.at[:, band(peer(k)), :], rs.at[k - 1], rs_snd.at[k - 1], rs_rcv.at[k - 1],
            {"tp": peer(k)},
        )
        for k in range(1, tp)
    ]
    ag_copies = [
        remote(
            full.at[:, band(col), :], full.at[:, band(col), :], ag_snd.at[k - 1],
            ag_rcv.at[k - 1], {"tp": peer(k)},
        )
        for k in range(1, tp)
    ]

    own_pairs()
    for c in rs_copies:
        c.start()
    attention()
    each(1, half + 1, lambda d: fac_copy(d).start())
    for c in rs_copies:
        c.wait_recv()
    total = ad[:, band(col), :].astype(F32)
    for k in range(1, tp):
        total = total + rs[k - 1].astype(F32)
    full[:, band(col), :] = total.astype(BF16)
    for c in ag_copies:
        c.start()
    for c in ag_copies:
        c.wait_recv()

    row_at = lax.broadcasted_iota(jnp.int32, (8, lanes), 0)
    lane_at = lax.broadcasted_iota(jnp.int32, (8, lanes), 1)

    def entry(d, other):
        b = dot(fac[:, width:], other[:, width:], NT)
        c = dot(fac[:, :width], other[:, :width], NT)
        product = full[2 * d].astype(F32) * b + full[2 * d + 1].astype(F32) * c
        return jnp.sum(jnp.sum(product, axis=0, keepdims=True), axis=1, keepdims=True)

    t1[...] = jnp.where((row_at == 0) & (lane_at == me), entry(0, fac), 0.0)

    def score(d):
        fac_copy(d).wait_recv()
        here = (lane_at == source(d)) & (row_at <= jnp.where(d < half, 1, 0))
        t1[...] += jnp.where(here, entry(d, fin.at[d - 1]), 0.0)

    each(1, half + 1, score)

    r1_copies = [
        remote(t1, t1_in.at[k - 1], r1_snd.at[k - 1], r1_rcv.at[k - 1], {"tp": peer(k)})
        for k in range(1, tp)
    ]
    for c in r1_copies:
        c.start()
    for c in r1_copies:
        c.wait_recv()
    whole = t1[...]
    for k in range(1, tp):
        whole = whole + t1_in[k - 1]
    t2[me] = whole

    def r2_copy(o):
        return remote(
            t2.at[me], t2.at[me], r2_snd.at[o - 1], r2_rcv.at[o - 1], {"seq": (me + o) % n}
        )

    each(1, n, lambda o: r2_copy(o).start())
    each(1, n, lambda o: r2_copy(o).wait_recv())

    straight, mirror = t2[:, 0, :], t2[:, 1, :]
    rank = lax.broadcasted_iota(jnp.int32, (n, lanes), 0)
    spot = lax.broadcasted_iota(jnp.int32, (n, lanes), 1)
    eye = rank == spot
    mine = jnp.sum(jnp.where(spot == me, mirror, 0.0), axis=1, keepdims=True)
    mirrored = jnp.sum(jnp.where(eye, mine, 0.0), axis=0, keepdims=True)
    own = jnp.sum(jnp.where(rank == me, straight, 0.0), axis=0, keepdims=True)
    diag = jnp.sum(jnp.where(eye, straight, 0.0), axis=0, keepdims=True)
    own_diag = jnp.sum(
        jnp.where(spot[:1] == me, diag, 0.0), axis=1, keepdims=True
    )
    gram = (own + mirrored) / jnp.sqrt(own_diag * diag)
    out_ref[...] = gram[:, :n]

    for k in order:
        for c in x_copies[k]:
            c.wait_send()
    for c in rs_copies + ag_copies + r1_copies:
        c.wait_send()

    def drain(d):
        for c in plane_copies(d):
            c.wait_send()
        fac_copy(d).wait_send()

    each(1, half + 1, drain)
    each(1, n, lambda o: r2_copy(o).wait_send())


def on_device(n, tp, states, cotangent, wq, wk, wv, wo):
    seq_dev, length, width = states.shape
    assert seq_dev == 1 and n % 2 == 0 and length == LANES
    kv = wk.shape[1]
    half = n // 2
    tiles = 2 * (half + 1)
    lanes = -(-n // LANES) * LANES
    cos, sin = rope_tables(length)
    vmem = pl.BlockSpec(memory_space=pltpu.VMEM)
    hbm = pl.BlockSpec(memory_space=pl.ANY)
    sem = pltpu.SemaphoreType.DMA
    return pl.pallas_call(
        functools.partial(kernel, n, tp),
        out_shape=jax.ShapeDtypeStruct((1, n), F32),
        in_specs=[vmem] * 4 + [hbm] * 4,
        out_specs=vmem,
        scratch_shapes=[
            pltpu.VMEM((tp - 1, length, width), BF16),
            pltpu.VMEM((tp - 1, length, width), BF16),
            pltpu.VMEM((tp, width, wq.shape[1]), BF16),
            pltpu.VMEM((tp, width, kv), BF16),
            pltpu.VMEM((tp, width, kv), BF16),
            pltpu.VMEM((tp, wo.shape[0], width), BF16),
            pltpu.VMEM((length, wq.shape[1]), F32),
            pltpu.VMEM((length, kv), F32),
            pltpu.VMEM((length, kv), F32),
            pltpu.VMEM((length, wo.shape[0]), F32),
            pltpu.VMEM((half, length, width), BF16),
            pltpu.VMEM((half, length, width), BF16),
            pltpu.VMEM((length, width + kv), BF16),
            pltpu.VMEM((half, length, width + kv), BF16),
            pltpu.VMEM((tiles, length, length), BF16),
            pltpu.VMEM((tp - 1, tiles, length // tp, length), BF16),
            pltpu.VMEM((tiles, length, length), BF16),
            pltpu.VMEM((8, lanes), F32),
            pltpu.VMEM((tp - 1, 8, lanes), F32),
            pltpu.VMEM((n, 8, lanes), F32),
            sem((4 * tp,)),
            sem((2, tp - 1)),
            sem((2, tp - 1)),
            sem((2, half)),
            sem((2, half)),
            sem((half,)),
            sem((half,)),
            sem((tp - 1,)),
            sem((tp - 1,)),
            sem((tp - 1,)),
            sem((tp - 1,)),
            sem((tp - 1,)),
            sem((tp - 1,)),
            sem((n - 1,)),
            sem((n - 1,)),
        ],
        compiler_params=pltpu.CompilerParams(
            collective_id=0, has_side_effects=True, vmem_limit_bytes=60 * 1024 * 1024
        ),
        name="ntk_gram",
    )(
        states.reshape(length, width), cotangent.reshape(length, width),
        jnp.asarray(cos), jnp.asarray(sin), wq, wk, wv, wo,
    )


def solution(mesh):
    in_specs = (
        P("seq", None, "tp"),
        P("seq", None, "tp"),
        P(None, "tp"),
        P(None, "tp"),
        P(None, "tp"),
        P("tp", None),
    )
    return jax.shard_map(
        functools.partial(on_device, mesh.shape["seq"], mesh.shape["tp"]),
        mesh=mesh, in_specs=in_specs, out_specs=P("seq", None), check_vma=False,
    )
```

time: 168 us -> 58 us (0.35)
  blocking collectives: 64.7 us -> 0 us
  Pallas kernels: 0 us -> 56.6 us
  waiting for transfers between devices: 43.4 us -> 0 us
  matrix products: 17.2 us -> 0 us
  between operations: 15.8 us -> 0.01 us
  local copies, waits for them, and re-layouts: 11.8 us -> 1.19 us
  other arithmetic: 9.77 us -> 0 us
  starting transfers between devices: 4.64 us -> 0 us
    pallas_call x0 -> x1, Pallas kernels: none -> 56.6 us  [on_device(): pl.pallas_call(functools.partial(kernel, n, tp), out_shape=jax.ShapeDtype...]
    all_gather x2 -> x0, blocking collectives: 34.1 us -> none  [the longest x1 17.7 us: attention_factors(): lax.all_gather(states, 'tp', axis=2, tiled=True)]
    unnamed x3 -> x0, waiting for transfers between devices: 34.1 us -> none
    dot_general x27 -> x0, matrix products: 17.2 us -> none  [the longest x20 10.4 us: tile_of(): lax.dot_general(left_rows[:, begin_col:end_col], right_rows[:, begin_col:...]
    unnamed x1 -> x0, blocking collectives: 11.8 us -> none
    psum x1 -> x0, blocking collectives: 10.7 us -> none  [on_device(): row_acc, col_acc = lax.psum((totals[0], totals[1]), 'tp')]
    ppermute x4 -> x0, waiting for transfers between devices: 9.32 us -> none  [from_behind(): return lax.ppermute(block, axis, route)]
    all_to_all x1 -> x0, blocking collectives: 8.08 us -> none  [on_device(): lax.all_to_all(col_acc, 'seq', split_axis=0, concat_axis=1, tiled=True)]
  transfers between devices with their start and end apart: 6 -> 0, of which waited for: 4 -> 0; matrix products, arithmetic and copies ran while one was open for 10% -> 0% of each run, Pallas kernels for 0% -> 0%
where the time goes in v1:
time: 58 us; the launch traced here: 57.8 us
  Pallas kernels  56.6 us (98%)
  local copies, waits for them, and re-layouts  1.19 us (2%)
    pallas_call x1, Pallas kernels, on_device(): pl.pallas_call(functools.partial(kernel, n, tp), out_shape=jax.ShapeDtype...  56.6 us
    unnamed x1, local copies, waits for them, and re-layouts  1.19 us

profile of v1, /device:TPU:0, one launch (start us, length us, event | category | flops | bytes accessed | tf_op | source)
XLA Modules:
  0.0 57.8 jit_solution(17542662524042349082)
XLA Ops:
  0.0 56.6 %ntk_gram.1 = f32[1,8]{1,0:T(1,128)} custom-call(bf16[128,512]{1,0:T(8,128)(2,1)} %bitcast.2, bf16[128,512]{1,0:T(8,128)(2,1)} %bitcast.3, f32[128,128]{1,0:T(8,128)} %constant.4.clone.cos_ref, f32[128,128]{1,0:T(8,128)} %constant.5.clone.sin_ref, bf16[2048,512]{1,0:T(8,128)(2,1)} %wq_hbm.1, bf16[2048,128]{1,0:T(8,128)(2,1)} %wk_hbm.1, ...), custom_call_target="tpu_custom_call" | custom-call | tf_op jit(solution)/shard_map/ntk_gram/pallas_call | solution.py:348
  56.7 1.2 %copy.10 = f32[1,8]{1,0:T(1,128)} copy(f32[1,8]{1,0:T(1,128)} %ntk_gram.1) | data formatting | bytes 64

commit v2 on v1

--- a/solution.py
+++ b/solution.py
@@ -59,8 +59,8 @@
     states_ref, cot_ref, cos_ref, sin_ref, wq_hbm, wk_hbm, wv_hbm, wo_hbm,
     out_ref,
     xs, cs, wqb, wkb, wvb, wob, q_acc, k_acc, v_acc, g_acc,
-    fs, fc, fac, fin, ad, rs, full, t1, t1_in, t2,
-    w_sem, x_snd, x_rcv, p_snd, p_rcv, f_snd, f_rcv,
+    fs, fc, att_own, att_in, gv_own, gv_in, probs, ad, rs, full, t1, t1_in, t2,
+    w_sem, x_snd, x_rcv, p_snd, p_rcv, a_snd, a_rcv, g_snd, g_rcv,
     rs_snd, rs_rcv, ag_snd, ag_rcv, r1_snd, r1_rcv, r2_snd, r2_rcv,
 ):
     length, width = states_ref.shape
@@ -116,16 +116,53 @@
             src_ref=src, dst_ref=dst, send_sem=snd, recv_sem=rcv, device_id=device
         )
 
-    order = sorted(range(1, tp), key=lambda k: min(k, tp - k))
-    x_copies = {}
-    for k in order:
-        to = {"tp": peer(k)}
-        x_copies[k] = (
-            remote(states_ref, xs.at[k - 1], x_snd.at[0, k - 1], x_rcv.at[0, k - 1], to),
-            remote(cot_ref, cs.at[k - 1], x_snd.at[1, k - 1], x_rcv.at[1, k - 1], to),
-        )
-        for c in x_copies[k]:
-            c.start()
+    inputs = (states_ref, cot_ref)
+    held = (xs, cs)
+
+    def up(which, k):
+        src = inputs[which] if k == 1 else held[which].at[k - 2]
+        return remote(
+            src, held[which].at[k - 1], x_snd.at[which, 0, k - 1], x_rcv.at[which, k - 1],
+            {"tp": peer(1)},
+        )
+
+    def down(which, k):
+        src = inputs[which] if k == 1 else held[which].at[tp - k]
+        return remote(
+            src, held[which].at[tp - k - 1], x_snd.at[which, 1, k - 1],
+            x_rcv.at[which, tp - k - 1], {"tp": peer(tp - 1)},
+        )
+
+    def sends_up(k):
+        return (col >= k - 1) & (col < tp - 1)
+
+    def sends_down(k):
+        return (col + k - 1 < tp) & (col > 0)
+
+    def pass_on(which, k, act):
+        @pl.when(sends_up(k))
+        def _():
+            act(up(which, k))
+
+        @pl.when(sends_down(k))
+        def _():
+            act(down(which, k))
+
+    def arrivals(k, body):
+        pl.when(col >= k)(lambda: body(k))
+        pl.when(col + k < tp)(lambda: body(tp - k))
+
+    def await_block(which, k):
+        arrivals(
+            k,
+            lambda slot: remote(
+                inputs[which], held[which].at[slot - 1], x_snd.at[which, 0, 0],
+                x_rcv.at[which, slot - 1], {"tp": peer(1)},
+            ).wait_recv(),
+        )
+
+    for which in range(2):
+        pass_on(which, 1, lambda c: c.start())
 
     def plane_copies(d):
         to = {"seq": target(d)}
@@ -140,25 +177,19 @@
 
     each(1, half + 1, start_plane)
 
-    for k in [0] + order:
-        for c in weight_copies[k]:
+    def project_states(slot):
+        for c in weight_copies[slot][:3]:
             c.wait()
-        if k == 0:
-            x, y = states_ref[...], cot_ref[...]
-        else:
-            for c in x_copies[k]:
-                c.wait_recv()
-            x, y = xs[k - 1], cs[k - 1]
-        for acc, piece in (
-            (q_acc, dot(x, wqb[k])),
-            (k_acc, dot(x, wkb[k])),
-            (v_acc, dot(x, wvb[k])),
-            (g_acc, dot(y, wob[k], NT)),
-        ):
-            if k == 0:
-                acc[...] = piece
-            else:
-                acc[...] += piece
+        x = states_ref[...] if slot == 0 else xs[slot - 1]
+        for acc, w in ((q_acc, wqb), (k_acc, wkb), (v_acc, wvb)):
+            piece = dot(x, w[slot])
+            acc[...] = piece if slot == 0 else acc[...] + piece
+
+    def project_cot(slot):
+        weight_copies[slot][3].wait()
+        y = cot_ref[...] if slot == 0 else cs[slot - 1]
+        piece = dot(y, wob[slot], NT)
+        g_acc[...] = piece if slot == 0 else g_acc[...] + piece
 
     lane = lax.broadcasted_iota(jnp.int32, (length, LANES), 1)
     low = lane < HEAD_DIM
@@ -185,39 +216,54 @@
             (jnp.where(low, other, zero).astype(BF16), jnp.where(low, zero, v).astype(BF16)),
         )
 
-    def attention():
-        for b in range(kv_cols // LANES):
-            kcut = slice(b * LANES, (b + 1) * LANES)
+    blocks = [
+        (b, g, (b * 2 + g) * (GROUP // 2) + pair)
+        for b in range(kv_cols // LANES)
+        for g in range(2)
+        for pair in range(GROUP // 2)
+    ]
+
+    def attend():
+        for b, g, at in blocks:
+            kcut, cut = slice(b * LANES, (b + 1) * LANES), slice(at * LANES, (at + 1) * LANES)
             keys = halves(rope(k_acc[:, kcut]))
             values = halves(v_acc[:, kcut])
-            sums = []
-            for g in range(2):
-                parts = [None, None]
-                for pair in range(GROUP // 2):
-                    at = ((b * 2 + g) * (GROUP // 2) + pair) * LANES
-                    cut = slice(at, at + LANES)
-                    q = rope(q_acc[:, cut]).astype(BF16)
-                    ga = g_acc[:, cut].astype(BF16)
-                    att = None
-                    for side in range(2):
-                        s = dot(q, keys[g][side], NT) * HEAD_DIM ** (-0.5)
-                        s = jnp.where(causal, s, -jnp.inf)
-                        e = jnp.exp(s - jnp.max(s, axis=1, keepdims=True))
-                        p = (e / jnp.sum(e, axis=1, keepdims=True)).astype(BF16)
-                        a = dot(p, values[g][side])
-                        att = a if att is None else att + a
-                        u = dot(p, ga, TN)
-                        parts[side] = u if parts[side] is None else parts[side] + u
-                    fac[:, cut] = att.astype(BF16)
-                sums.append(parts)
+            q = rope(q_acc[:, cut]).astype(BF16)
+            att = None
+            for side in range(2):
+                s = dot(q, keys[g][side], NT) * HEAD_DIM ** (-0.5)
+                s = jnp.where(causal, s, -jnp.inf)
+                e = jnp.exp(s - jnp.max(s, axis=1, keepdims=True))
+                p = (e / jnp.sum(e, axis=1, keepdims=True)).astype(BF16)
+                probs[2 * at + side] = p
+                a = dot(p, values[g][side])
+                att = a if att is None else att + a
+            att_own[:, cut] = att.astype(BF16)
+
+    def grad_values():
+        sums = {}
+        for b, g, at in blocks:
+            ga = g_acc[:, at * LANES : (at + 1) * LANES].astype(BF16)
+            for side in range(2):
+                u = dot(probs[2 * at + side], ga, TN)
+                key = (b, g, side)
+                sums[key] = sums[key] + u if key in sums else u
+        for b in range(kv_cols // LANES):
             grad = jnp.where(
-                low, sums[0][0] + swap(sums[0][1]), swap(sums[1][0]) + sums[1][1]
+                low,
+                sums[b, 0, 0] + swap(sums[b, 0, 1]),
+                swap(sums[b, 1, 0]) + sums[b, 1, 1],
             )
-            fac[:, width + b * LANES : width + (b + 1) * LANES] = grad.astype(BF16)
-
-    def fac_copy(d):
+            gv_own[:, b * LANES : (b + 1) * LANES] = grad.astype(BF16)
+
+    def att_copy(d):
         return remote(
-            fac, fin.at[d - 1], f_snd.at[d - 1], f_rcv.at[d - 1], {"seq": target(d)}
+            att_own, att_in.at[d - 1], a_snd.at[d - 1], a_rcv.at[d - 1], {"seq": target(d)}
+        )
+
+    def gv_copy(d):
+        return remote(
+            gv_own, gv_in.at[d - 1], g_snd.at[d - 1], g_rcv.at[d - 1], {"seq": target(d)}
         )
 
     def band(k):
@@ -250,11 +296,27 @@
         for k in range(1, tp)
     ]
 
-    own_pairs()
-    for c in rs_copies:
-        c.start()
-    attention()
-    each(1, half + 1, lambda d: fac_copy(d).start())
+    project_states(0)
+    project_cot(0)
+    for k in range(1, tp):
+        if k == tp - 1:
+            own_pairs()
+            for c in rs_copies:
+                c.start()
+        await_block(0, k)
+        if k < tp - 1:
+            pass_on(0, k + 1, lambda c: c.start())
+        arrivals(k, project_states)
+        if k == tp - 1:
+            attend()
+            each(1, half + 1, lambda d: att_copy(d).start())
+        await_block(1, k)
+        if k < tp - 1:
+            pass_on(1, k + 1, lambda c: c.start())
+        arrivals(k, project_cot)
+    grad_values()
+    each(1, half + 1, lambda d: gv_copy(d).start())
+
     for c in rs_copies:
         c.wait_recv()
     total = ad[:, band(col), :].astype(F32)
@@ -269,18 +331,19 @@
     row_at = lax.broadcasted_iota(jnp.int32, (8, lanes), 0)
     lane_at = lax.broadcasted_iota(jnp.int32, (8, lanes), 1)
 
-    def entry(d, other):
-        b = dot(fac[:, width:], other[:, width:], NT)
-        c = dot(fac[:, :width], other[:, :width], NT)
+    def entry(d, att_other, gv_other):
+        b = dot(gv_own[...], gv_other[...], NT)
+        c = dot(att_own[...], att_other[...], NT)
         product = full[2 * d].astype(F32) * b + full[2 * d + 1].astype(F32) * c
         return jnp.sum(jnp.sum(product, axis=0, keepdims=True), axis=1, keepdims=True)
 
-    t1[...] = jnp.where((row_at == 0) & (lane_at == me), entry(0, fac), 0.0)
+    t1[...] = jnp.where((row_at == 0) & (lane_at == me), entry(0, att_own, gv_own), 0.0)
 
     def score(d):
-        fac_copy(d).wait_recv()
+        att_copy(d).wait_recv()
+        gv_copy(d).wait_recv()
         here = (lane_at == source(d)) & (row_at <= jnp.where(d < half, 1, 0))
-        t1[...] += jnp.where(here, entry(d, fin.at[d - 1]), 0.0)
+        t1[...] += jnp.where(here, entry(d, att_in.at[d - 1], gv_in.at[d - 1]), 0.0)
 
     each(1, half + 1, score)
 
@@ -319,16 +382,17 @@
     gram = (own + mirrored) / jnp.sqrt(own_diag * diag)
     out_ref[...] = gram[:, :n]
 
-    for k in order:
-        for c in x_copies[k]:
-            c.wait_send()
+    for k in range(1, tp):
+        for which in range(2):
+            pass_on(which, k, lambda c: c.wait_send())
     for c in rs_copies + ag_copies + r1_copies:
         c.wait_send()
 
     def drain(d):
         for c in plane_copies(d):
             c.wait_send()
-        fac_copy(d).wait_send()
+        att_copy(d).wait_send()
+        gv_copy(d).wait_send()
 
     each(1, half + 1, drain)
     each(1, n, lambda o: r2_copy(o).wait_send())
@@ -363,8 +427,11 @@
             pltpu.VMEM((length, wo.shape[0]), F32),
             pltpu.VMEM((half, length, width), BF16),
             pltpu.VMEM((half, length, width), BF16),
-            pltpu.VMEM((length, width + kv), BF16),
-            pltpu.VMEM((half, length, width + kv), BF16),
+            pltpu.VMEM((length, width), BF16),
+            pltpu.VMEM((half, length, width), BF16),
+            pltpu.VMEM((length, kv), BF16),
+            pltpu.VMEM((half, length, kv), BF16),
+            pltpu.VMEM((width // HEAD_DIM, length, length), BF16),
             pltpu.VMEM((tiles, length, length), BF16),
             pltpu.VMEM((tp - 1, tiles, length // tp, length), BF16),
             pltpu.VMEM((tiles, length, length), BF16),
@@ -372,10 +439,12 @@
             pltpu.VMEM((tp - 1, 8, lanes), F32),
             pltpu.VMEM((n, 8, lanes), F32),
             sem((4 * tp,)),
-            sem((2, tp - 1)),
+            sem((2, 2, tp - 1)),
             sem((2, tp - 1)),
             sem((2, half)),
             sem((2, half)),
+            sem((half,)),
+            sem((half,)),
             sem((half,)),
             sem((half,)),
             sem((tp - 1,)),

time: 58 us -> 51.1 us (0.88)
  Pallas kernels: 56.6 us -> 49.8 us
    pallas_call x1, Pallas kernels: 56.6 us -> 49.8 us  [on_device(): pl.pallas_call(functools.partial(kernel, n, tp), out_shape=jax.ShapeDtype...]
where the time goes in v2:
time: 51.1 us; the launch traced here: 51 us
  Pallas kernels  49.8 us (97%)
  local copies, waits for them, and re-layouts  1.19 us (2%)
    pallas_call x1, Pallas kernels, on_device(): pl.pallas_call(functools.partial(kernel, n, tp), out_shape=jax.ShapeDtype...  49.8 us
    unnamed x1, local copies, waits for them, and re-layouts  1.19 us

profile of v2, /device:TPU:0, one launch (start us, length us, event | category | flops | bytes accessed | tf_op | source)
XLA Modules:
  0.0 51.0 jit_solution(11387422389456195190)
XLA Ops:
  0.0 49.8 %ntk_gram.1 = f32[1,8]{1,0:T(1,128)} custom-call(bf16[128,512]{1,0:T(8,128)(2,1)} %bitcast.2, bf16[128,512]{1,0:T(8,128)(2,1)} %bitcast.3, f32[128,128]{1,0:T(8,128)} %constant.4.clone.cos_ref, f32[128,128]{1,0:T(8,128)} %constant.5.clone.sin_ref, bf16[2048,512]{1,0:T(8,128)(2,1)} %wq_hbm.1, bf16[2048,128]{1,0:T(8,128)(2,1)} %wk_hbm.1, ...), custom_call_target="tpu_custom_call" | custom-call | tf_op jit(solution)/shard_map/ntk_gram/pallas_call | solution.py:412
  49.8 1.2 %copy.10 = f32[1,8]{1,0:T(1,128)} copy(f32[1,8]{1,0:T(1,128)} %ntk_gram.1) | data formatting | bytes 64

commit v3 on v2

--- a/solution.py
+++ b/solution.py
@@ -59,15 +59,15 @@
     states_ref, cot_ref, cos_ref, sin_ref, wq_hbm, wk_hbm, wv_hbm, wo_hbm,
     out_ref,
     xs, cs, wqb, wkb, wvb, wob, q_acc, k_acc, v_acc, g_acc,
-    fs, fc, att_own, att_in, gv_own, gv_in, probs, ad, rs, full, t1, t1_in, t2,
+    fs, fc, att_own, att_in, gv_own, gv_in, probs, ad, rs, full, t2,
     w_sem, x_snd, x_rcv, p_snd, p_rcv, a_snd, a_rcv, g_snd, g_rcv,
-    rs_snd, rs_rcv, ag_snd, ag_rcv, r1_snd, r1_rcv, r2_snd, r2_rcv,
+    rs_snd, rs_rcv, ag_snd, ag_rcv, r2_snd, r2_rcv,
 ):
     length, width = states_ref.shape
     kv_cols = k_acc.shape[1]
     half = n // 2
     rows = length // tp
-    lanes = t1.shape[1]
+    lanes = t2.shape[3]
     me = lax.axis_index("seq")
     col = lax.axis_index("tp")
     place = place_of(me, n)
@@ -269,67 +269,72 @@
     def band(k):
         return pl.ds(pl.multiple_of(k * rows, rows), rows)
 
-    def own_pairs():
-        ad[0] = dot(states_ref[...], states_ref[...], NT).astype(BF16)
-        ad[1] = dot(cot_ref[...], cot_ref[...], NT).astype(BF16)
-
-        def pair(d):
-            for c in plane_copies(d):
-                c.wait_recv()
-            ad[2 * d] = dot(states_ref[...], fs[d - 1], NT).astype(BF16)
-            ad[2 * d + 1] = dot(cot_ref[...], fc[d - 1], NT).astype(BF16)
-
-        each(1, half + 1, pair)
-
-    rs_copies = [
-        remote(
-            ad.at[:, band(peer(k)), :], rs.at[k - 1], rs_snd.at[k - 1], rs_rcv.at[k - 1],
-            {"tp": peer(k)},
-        )
-        for k in range(1, tp)
-    ]
-    ag_copies = [
-        remote(
-            full.at[:, band(col), :], full.at[:, band(col), :], ag_snd.at[k - 1],
-            ag_rcv.at[k - 1], {"tp": peer(k)},
-        )
-        for k in range(1, tp)
-    ]
+    def rs_copies(d):
+        two = pl.ds(2 * d, 2)
+        return [
+            remote(
+                ad.at[two, band(peer(k)), :], rs.at[k - 1, two], rs_snd.at[k - 1, d],
+                rs_rcv.at[k - 1, d], {"tp": peer(k)},
+            )
+            for k in range(1, tp)
+        ]
+
+    def ag_copies(d):
+        part = full.at[pl.ds(2 * d, 2), band(col), :]
+        return [
+            remote(part, part, ag_snd.at[k - 1, d], ag_rcv.at[k - 1, d], {"tp": peer(k)})
+            for k in range(1, tp)
+        ]
+
+    def multiply(d, states_other, cot_other):
+        ad[2 * d] = dot(states_ref[...], states_other[...], NT).astype(BF16)
+        ad[2 * d + 1] = dot(cot_ref[...], cot_other[...], NT).astype(BF16)
+        for c in rs_copies(d):
+            c.start()
+
+    def pair(d):
+        for c in plane_copies(d):
+            c.wait_recv()
+        multiply(d, fs.at[d - 1], fc.at[d - 1])
+
+    def gather_sum(d):
+        for c in rs_copies(d):
+            c.wait_recv()
+        two = pl.ds(2 * d, 2)
+        total = ad[two, band(col), :].astype(F32)
+        for k in range(1, tp):
+            total = total + rs[k - 1, two].astype(F32)
+        full[two, band(col), :] = total.astype(BF16)
+        for c in ag_copies(d):
+            c.start()
+
+    bounds = [1 + (half * k + tp - 2) // (tp - 1) for k in range(tp)]
 
     project_states(0)
+    multiply(0, states_ref, cot_ref)
     project_cot(0)
     for k in range(1, tp):
-        if k == tp - 1:
-            own_pairs()
-            for c in rs_copies:
-                c.start()
+        last = k == tp - 1
         await_block(0, k)
-        if k < tp - 1:
+        if not last:
             pass_on(0, k + 1, lambda c: c.start())
         arrivals(k, project_states)
-        if k == tp - 1:
+        if last:
+            each(bounds[k - 1], bounds[k], pair)
             attend()
             each(1, half + 1, lambda d: att_copy(d).start())
         await_block(1, k)
-        if k < tp - 1:
+        if not last:
             pass_on(1, k + 1, lambda c: c.start())
         arrivals(k, project_cot)
+        if not last:
+            each(bounds[k - 1], bounds[k], pair)
+            each(bounds[k - 2] if k > 1 else 0, bounds[k - 1], gather_sum)
     grad_values()
     each(1, half + 1, lambda d: gv_copy(d).start())
-
-    for c in rs_copies:
-        c.wait_recv()
-    total = ad[:, band(col), :].astype(F32)
-    for k in range(1, tp):
-        total = total + rs[k - 1].astype(F32)
-    full[:, band(col), :] = total.astype(BF16)
-    for c in ag_copies:
-        c.start()
-    for c in ag_copies:
-        c.wait_recv()
-
-    row_at = lax.broadcasted_iota(jnp.int32, (8, lanes), 0)
-    lane_at = lax.broadcasted_iota(jnp.int32, (8, lanes), 1)
+    each(bounds[tp - 3] if tp > 2 else 0, bounds[tp - 1], gather_sum)
+
+    lane_at = lax.broadcasted_iota(jnp.int32, (1, lanes), 1)
 
     def entry(d, att_other, gv_other):
         b = dot(gv_own[...], gv_other[...], NT)
@@ -337,56 +342,61 @@
         product = full[2 * d].astype(F32) * b + full[2 * d + 1].astype(F32) * c
         return jnp.sum(jnp.sum(product, axis=0, keepdims=True), axis=1, keepdims=True)
 
-    t1[...] = jnp.where((row_at == 0) & (lane_at == me), entry(0, att_own, gv_own), 0.0)
+    def settle(d):
+        for c in ag_copies(d):
+            c.wait_recv()
+
+    settle(0)
+    t2[col, me] = jnp.where(lane_at == me, entry(0, att_own, gv_own), 0.0)
 
     def score(d):
+        settle(d)
         att_copy(d).wait_recv()
         gv_copy(d).wait_recv()
-        here = (lane_at == source(d)) & (row_at <= jnp.where(d < half, 1, 0))
-        t1[...] += jnp.where(here, entry(d, att_in.at[d - 1], gv_in.at[d - 1]), 0.0)
+        value = entry(d, att_in.at[d - 1], gv_in.at[d - 1])
+        t2[col, me] += jnp.where(lane_at == source(d), value, 0.0)
 
     each(1, half + 1, score)
 
-    r1_copies = [
-        remote(t1, t1_in.at[k - 1], r1_snd.at[k - 1], r1_rcv.at[k - 1], {"tp": peer(k)})
-        for k in range(1, tp)
-    ]
-    for c in r1_copies:
-        c.start()
-    for c in r1_copies:
-        c.wait_recv()
-    whole = t1[...]
-    for k in range(1, tp):
-        whole = whole + t1_in[k - 1]
-    t2[me] = whole
-
     def r2_copy(o):
-        return remote(
-            t2.at[me], t2.at[me], r2_snd.at[o - 1], r2_rcv.at[o - 1], {"seq": (me + o) % n}
-        )
-
-    each(1, n, lambda o: r2_copy(o).start())
-    each(1, n, lambda o: r2_copy(o).wait_recv())
-
-    straight, mirror = t2[:, 0, :], t2[:, 1, :]
+        mine = t2.at[col, me]
+        to = {"seq": (me + o) % n, "tp": (col + o // n) % tp}
+        return remote(mine, mine, r2_snd.at[o - 1], r2_rcv.at[o - 1], to)
+
+    def every(act):
+        if n * tp <= 32:
+            for o in range(1, n * tp):
+                act(r2_copy(o))
+        else:
+            each(1, n * tp, lambda o: act(r2_copy(o)))
+
+    every(lambda c: c.start())
+    every(lambda c: c.wait_recv())
+
+    table = t2[0].reshape(n, lanes)
+    for q in range(1, tp):
+        table = table + t2[q].reshape(n, lanes)
     rank = lax.broadcasted_iota(jnp.int32, (n, lanes), 0)
     spot = lax.broadcasted_iota(jnp.int32, (n, lanes), 1)
     eye = rank == spot
-    mine = jnp.sum(jnp.where(spot == me, mirror, 0.0), axis=1, keepdims=True)
-    mirrored = jnp.sum(jnp.where(eye, mine, 0.0), axis=0, keepdims=True)
-    own = jnp.sum(jnp.where(rank == me, straight, 0.0), axis=0, keepdims=True)
-    diag = jnp.sum(jnp.where(eye, straight, 0.0), axis=0, keepdims=True)
-    own_diag = jnp.sum(
-        jnp.where(spot[:1] == me, diag, 0.0), axis=1, keepdims=True
-    )
+    column = jnp.sum(jnp.where(spot == me, table, 0.0), axis=1, keepdims=True)
+    theirs = eye & (rank != me) & (rank != source(half))
+    mirrored = jnp.sum(jnp.where(theirs, column, 0.0), axis=0, keepdims=True)
+    own = jnp.sum(jnp.where(rank == me, table, 0.0), axis=0, keepdims=True)
+    diag = jnp.sum(jnp.where(eye, table, 0.0), axis=0, keepdims=True)
+    own_diag = jnp.sum(jnp.where(lane_at == me, diag, 0.0), axis=1, keepdims=True)
     gram = (own + mirrored) / jnp.sqrt(own_diag * diag)
     out_ref[...] = gram[:, :n]
 
     for k in range(1, tp):
         for which in range(2):
             pass_on(which, k, lambda c: c.wait_send())
-    for c in rs_copies + ag_copies + r1_copies:
-        c.wait_send()
+
+    def drain_sums(d):
+        for c in rs_copies(d) + ag_copies(d):
+            c.wait_send()
+
+    each(0, half + 1, drain_sums)
 
     def drain(d):
         for c in plane_copies(d):
@@ -395,7 +405,7 @@
         gv_copy(d).wait_send()
 
     each(1, half + 1, drain)
-    each(1, n, lambda o: r2_copy(o).wait_send())
+    every(lambda c: c.wait_send())
 
 
 def on_device(n, tp, states, cotangent, wq, wk, wv, wo):
@@ -435,9 +445,7 @@
             pltpu.VMEM((tiles, length, length), BF16),
             pltpu.VMEM((tp - 1, tiles, length // tp, length), BF16),
             pltpu.VMEM((tiles, length, length), BF16),
-            pltpu.VMEM((8, lanes), F32),
-            pltpu.VMEM((tp - 1, 8, lanes), F32),
-            pltpu.VMEM((n, 8, lanes), F32),
+            pltpu.VMEM((tp, n, 1, lanes), F32),
             sem((4 * tp,)),
             sem((2, 2, tp - 1)),
             sem((2, tp - 1)),
@@ -447,14 +455,12 @@
             sem((half,)),
             sem((half,)),
             sem((half,)),
-            sem((tp - 1,)),
-            sem((tp - 1,)),
-            sem((tp - 1,)),
-            sem((tp - 1,)),
-            sem((tp - 1,)),
-            sem((tp - 1,)),
-            sem((n - 1,)),
-            sem((n - 1,)),
+            sem((tp - 1, half + 1)),
+            sem((tp - 1, half + 1)),
+            sem((tp - 1, half + 1)),
+            sem((tp - 1, half + 1)),
+            sem((n * tp - 1,)),
+            sem((n * tp - 1,)),
         ],
         compiler_params=pltpu.CompilerParams(
             collective_id=0, has_side_effects=True, vmem_limit_bytes=60 * 1024 * 1024

time: 51.1 us -> 49.1 us (0.961)
  Pallas kernels: 49.8 us -> 47.8 us
    pallas_call x1, Pallas kernels: 49.8 us -> 47.8 us  [on_device(): pl.pallas_call(functools.partial(kernel, n, tp), out_shape=jax.ShapeDtype...]
where the time goes in v3:
time: 49.1 us; the launch traced here: 49 us
  Pallas kernels  47.8 us (97%)
  local copies, waits for them, and re-layouts  1.19 us (2%)
    pallas_call x1, Pallas kernels, on_device(): pl.pallas_call(functools.partial(kernel, n, tp), out_shape=jax.ShapeDtype...  47.8 us
    unnamed x1, local copies, waits for them, and re-layouts  1.19 us

profile of v3, /device:TPU:0, one launch (start us, length us, event | category | flops | bytes accessed | tf_op | source)
XLA Modules:
  0.0 49.0 jit_solution(18107821574714128132)
XLA Ops:
  0.0 47.8 %ntk_gram.1 = f32[1,8]{1,0:T(1,128)} custom-call(bf16[128,512]{1,0:T(8,128)(2,1)} %bitcast.2, bf16[128,512]{1,0:T(8,128)(2,1)} %bitcast.3, f32[128,128]{1,0:T(8,128)} %constant.4.clone.cos_ref, f32[128,128]{1,0:T(8,128)} %constant.5.clone.sin_ref, bf16[2048,512]{1,0:T(8,128)(2,1)} %wq_hbm.1, bf16[2048,128]{1,0:T(8,128)(2,1)} %wk_hbm.1, ...), custom_call_target="tpu_custom_call" | custom-call | tf_op jit(solution)/shard_map/ntk_gram/pallas_call | solution.py:422
  47.8 1.2 %copy.10 = f32[1,8]{1,0:T(1,128)} copy(f32[1,8]{1,0:T(1,128)} %ntk_gram.1) | data formatting | bytes 64

commit v4 on v3

--- a/solution.py
+++ b/solution.py
@@ -223,8 +223,11 @@
         for pair in range(GROUP // 2)
     ]
 
-    def attend():
-        for b, g, at in blocks:
+    part_cols = width // 2
+
+    def attend(part):
+        share = len(blocks) // 2
+        for b, g, at in blocks[part * share : (part + 1) * share]:
             kcut, cut = slice(b * LANES, (b + 1) * LANES), slice(at * LANES, (at + 1) * LANES)
             keys = halves(rope(k_acc[:, kcut]))
             values = halves(v_acc[:, kcut])
@@ -256,9 +259,11 @@
             )
             gv_own[:, b * LANES : (b + 1) * LANES] = grad.astype(BF16)
 
-    def att_copy(d):
+    def att_copy(d, part):
+        cut = pl.ds(part * part_cols, part_cols)
         return remote(
-            att_own, att_in.at[d - 1], a_snd.at[d - 1], a_rcv.at[d - 1], {"seq": target(d)}
+            att_own.at[:, cut], att_in.at[d - 1, :, cut], a_snd.at[part, d - 1],
+            a_rcv.at[part, d - 1], {"seq": target(d)},
         )
 
     def gv_copy(d):
@@ -321,8 +326,10 @@
         arrivals(k, project_states)
         if last:
             each(bounds[k - 1], bounds[k], pair)
-            attend()
-            each(1, half + 1, lambda d: att_copy(d).start())
+            for part in range(2):
+                attend(part)
+                each(1, half + 1, lambda d: att_copy(d, part).start())
+            each(bounds[k - 2] if k > 1 else 0, bounds[k], gather_sum)
         await_block(1, k)
         if not last:
             pass_on(1, k + 1, lambda c: c.start())
@@ -332,7 +339,6 @@
             each(bounds[k - 2] if k > 1 else 0, bounds[k - 1], gather_sum)
     grad_values()
     each(1, half + 1, lambda d: gv_copy(d).start())
-    each(bounds[tp - 3] if tp > 2 else 0, bounds[tp - 1], gather_sum)
 
     lane_at = lax.broadcasted_iota(jnp.int32, (1, lanes), 1)
 
@@ -351,7 +357,8 @@
 
     def score(d):
         settle(d)
-        att_copy(d).wait_recv()
+        for part in range(2):
+            att_copy(d, part).wait_recv()
         gv_copy(d).wait_recv()
         value = entry(d, att_in.at[d - 1], gv_in.at[d - 1])
         t2[col, me] += jnp.where(lane_at == source(d), value, 0.0)
@@ -401,7 +408,8 @@
     def drain(d):
         for c in plane_copies(d):
             c.wait_send()
-        att_copy(d).wait_send()
+        for part in range(2):
+            att_copy(d, part).wait_send()
         gv_copy(d).wait_send()
 
     each(1, half + 1, drain)
@@ -451,8 +459,8 @@
             sem((2, tp - 1)),
             sem((2, half)),
             sem((2, half)),
-            sem((half,)),
-            sem((half,)),
+            sem((2, half)),
+            sem((2, half)),
             sem((half,)),
             sem((half,)),
             sem((tp - 1, half + 1)),

time: 49.1 us -> 48.1 us (0.980)
  Pallas kernels: 47.8 us -> 46.7 us
    pallas_call x1, Pallas kernels: 47.8 us -> 46.7 us  [on_device(): pl.pallas_call(functools.partial(kernel, n, tp), out_shape=jax.ShapeDtype...]
where the time goes in v4:
time: 48.1 us; the launch traced here: 47.9 us
  Pallas kernels  46.7 us (97%)
  local copies, waits for them, and re-layouts  1.19 us (2%)
    pallas_call x1, Pallas kernels, on_device(): pl.pallas_call(functools.partial(kernel, n, tp), out_shape=jax.ShapeDtype...  46.7 us
    unnamed x1, local copies, waits for them, and re-layouts  1.19 us

profile of v4, /device:TPU:0, one launch (start us, length us, event | category | flops | bytes accessed | tf_op | source)
XLA Modules:
  0.0 47.9 jit_solution(10302723042549222579)
XLA Ops:
  0.0 46.7 %ntk_gram.1 = f32[1,8]{1,0:T(1,128)} custom-call(bf16[128,512]{1,0:T(8,128)(2,1)} %bitcast.2, bf16[128,512]{1,0:T(8,128)(2,1)} %bitcast.3, f32[128,128]{1,0:T(8,128)} %constant.4.clone.cos_ref, f32[128,128]{1,0:T(8,128)} %constant.5.clone.sin_ref, bf16[2048,512]{1,0:T(8,128)(2,1)} %wq_hbm.1, bf16[2048,128]{1,0:T(8,128)(2,1)} %wk_hbm.1, ...), custom_call_target="tpu_custom_call" | custom-call | tf_op jit(solution)/shard_map/ntk_gram/pallas_call | solution.py:430
  46.7 1.2 %copy.10 = f32[1,8]{1,0:T(1,128)} copy(f32[1,8]{1,0:T(1,128)} %ntk_gram.1) | data formatting | bytes 64
